TPU v7x, 256 devices: a whole 4x4x8 slice. The times are simulated.
256 devices in a mesh: rep: 1, dp: 256 (over x, y, z, core).
Axes of the slice: x: 4, y: 4, z: 8, core: 2. Of those that a mesh axis runs over, the one named last changes fastest.
Arguments:
- x: bfloat16 [256, 1024, 768], P(('rep', 'dp'))
- dy: bfloat16 [256, 1024, 768], P(('rep', 'dp'))
- w_gate: bfloat16 [2, 768, 2048], replicated
- w_up: bfloat16 [2, 768, 2048], replicated
- w_down: bfloat16 [2, 2048, 768], replicated
- m_w_gate: float32 [2, 768, 2048], replicated
- m_w_up: float32 [2, 768, 2048], replicated
- m_w_down: float32 [2, 2048, 768], replicated
- v_w_gate: float32 [2, 768, 2048], replicated
- v_w_up: float32 [2, 768, 2048], replicated
- v_w_down: float32 [2, 2048, 768], replicated
Outputs:
- output 1: bfloat16 [2, 768, 2048], P('rep')
- output 2: bfloat16 [2, 768, 2048], P('rep')
- output 3: bfloat16 [2, 2048, 768], P('rep')
- output 4: float32 [2, 768, 2048], P('rep')
- output 5: float32 [2, 768, 2048], P('rep')
- output 6: float32 [2, 2048, 768], P('rep')
- output 7: float32 [2, 768, 2048], P('rep')
- output 8: float32 [2, 768, 2048], P('rep')
- output 9: float32 [2, 2048, 768], P('rep')
All inputs are finite; a program needn't handle non-finite values.
Results may differ from a plain program's by a relative error of at most 0.022.
Values are sent between devices in bfloat16 or wider.
A program may use at most 768 MiB of HBM per device.

v0:
```python
import functools

import jax
import jax.numpy as jnp
from jax import lax
from jax.experimental import pallas as pl
from jax.experimental.pallas import tpu as pltpu
from jax.sharding import PartitionSpec as P

F32, BF16 = jnp.float32, jnp.bfloat16
MESH = pl.DeviceIdType.MESH
SLOTS = 8
W = 256
LANES = 128


class Plan:
    def __init__(self, sizes, tiles, half):
        self.sizes, self.tiles, self.half = sizes, tiles, half
        nx, ny, nz = sizes
        self.axes = ((0, 1, 2), (1, 0, 2), (2, 0, 1))
        self.chunk = tuple(half // sizes[a[0]] for a in self.axes)
        self.piece = (half // (nx * ny), half // (nx * ny), 2 * half // (nz * nx))


STAGES = ("core", "r1", "r2", "r3", "r4", "p2", "p3", "b3", "b2", "a1", "a2", "a3", "a4", "out")


def rem(a, b):
    return lax.rem(a, jnp.int32(b))


def div(a, b):
    return lax.div(a, jnp.int32(b))


def dot(a, b, dims=((1,), (0,))):
    return lax.dot_general(a, b, (dims, ((), ())), preferred_element_type=F32)


LAST = ((1,), (1,))


def normed(h):
    wide = h.astype(F32)
    return (wide * lax.rsqrt(jnp.mean(wide * wide, -1, keepdims=True) + 1e-6)).astype(BF16)


def train_kernel(plan, *refs):
    sizes, tiles, half = plan.sizes, plan.tiles, plan.half
    x_hbm, dy_hbm, gate_hbm, up_hbm, down_hbm = refs[:5]
    g_out, squares = refs[5:7]
    scratch = list(refs[7:])

    def take(count):
        out, scratch[:] = scratch[:count], scratch[count:]
        return out

    g, mine, taken, s = take(4)
    ring_in, ring_out, pair_in, pair_out, kept, own_in, own_out, own_kept = (take(3) for _ in range(8))
    sq, = take(1)
    recv, send, out_sem, sq_recv, sq_send_sem = take(5)
    h, d, a0, a1, at_, dt, acc, p, dg, du, down_all, wg, wu, wd, in_sem, w_sem = take(16)
    tokens, width = h.shape
    per = tiles // 2
    rows = min(256, tokens)

    me = lax.axis_index("dp")
    core = rem(me, 2)
    at = [div(me, 2 * sizes[1] * sizes[2]), rem(div(me, 2 * sizes[2]), sizes[1]), rem(div(me, 2), sizes[2])]
    way = 1 - 2 * core

    def device(axis=None, place=None, other_core=False):
        c = [place if a == axis else at[a] for a in range(3)]
        return {"dp": ((c[0] * sizes[1] + c[1]) * sizes[2] + c[2]) * 2 + ((1 - core) if other_core else core)}

    def along(axis, step):
        return rem(at[axis] + step + 2 * sizes[axis], sizes[axis])


    def fetch(layer, t, slot, start, down=True):
        cols = pl.ds(pl.multiple_of(t * W, W), W)
        copies = [(gate_hbm.at[layer, :, cols], wg.at[slot]), (up_hbm.at[layer, :, cols], wu.at[slot])]
        if down:
            copies.append((down_hbm.at[layer, cols, :], wd.at[slot]))
        for i, (src, dst) in enumerate(copies):
            copy = pltpu.make_async_copy(src, dst, w_sem.at[slot, i])
            copy.start() if start else copy.wait()

    def fetch_tile(q, start):
        for layer in range(2):
            first = (1 - layer) * per

            @pl.when((q >= first) & (q < first + per))
            def _():
                fetch(layer, q - first, rem(q, 4), start)

    def tile_forward(slot, a, d):
        for r in range(0, tokens, rows):
            block = pl.ds(r, rows)
            gate = dot(a[block, :], wg[slot])
            up = dot(a[block, :], wu[slot])
            by_p = dot(d[block, :], wd[slot], LAST).astype(BF16).astype(F32)
            sig = jax.nn.sigmoid(gate)
            act = gate * sig
            p[block, 0:W] = (act * up).astype(BF16)
            du[block, :] = (by_p * act).astype(BF16)
            dg[block, :] = (by_p * up * (sig * (1 + gate * (1 - sig)))).astype(BF16)

    def tile_gradients(tile, dt):
        for color, (left, right) in enumerate(((at_, dg), (at_, du), (dt, p))):
            out = dot(left[...], right[:, 0:W])
            low, high = out[:, :LANES], out[:, LANES:]
            s[rem(tile, S_SLOTS), color] = jnp.where(core == 0, low, high)
            mine[rem(tile, 2), color] = jnp.where(core == 0, high, low).astype(BF16)

    def tile_by_input(slot):
        for r in range(0, tokens, rows):
            block = pl.ds(r, rows)
            acc[block, :] += dot(dg[block, :], wg[slot], LAST) + dot(du[block, :], wu[slot], LAST)

    def through_norm():
        for r in range(0, tokens, rows):
            block = pl.ds(r, rows)
            wide = h[block, :].astype(F32)
            scale = lax.rsqrt(jnp.mean(wide * wide, -1, keepdims=True) + 1e-6)
            by_a = acc[block, :].astype(BF16).astype(F32)
            by_h = by_a * scale - wide * (scale * scale * scale * (jnp.sum(by_a * wide, -1, keepdims=True) * (1.0 / width)))
            d[block, :] = (d[block, :].astype(F32) + by_h.astype(BF16).astype(F32)).astype(BF16)

    def forward():
        load_x = pltpu.make_async_copy(x_hbm.at[0], h, in_sem.at[0])
        load_dy = pltpu.make_async_copy(dy_hbm.at[0], d, in_sem.at[1])
        load_down = pltpu.make_async_copy(down_hbm.at[0], down_all, in_sem.at[2])
        load_x.start()
        for t in range(2):
            fetch(0, t, t, True, False)
        load_down.start()
        load_dy.start()
        load_x.wait()
        for r in range(0, tokens, rows):
            a0[r : r + rows, :] = normed(h[r : r + rows, :])

        def pair(i, carry):
            base = 2 * rem(i, 2)
            for k in range(2):
                fetch(0, 2 * i + k, base + k, False, False)

            @pl.when(i + 1 < per // 2)
            def _():
                for k in range(2):
                    fetch(0, 2 * i + 2 + k, 2 - base + k, True, False)

            @pl.when(i + 1 == per // 2)
            def _():
                fetch(1, 0, 2 - base, True)

            for k in range(2):
                for r in range(0, tokens, rows):
                    gate = dot(a0[r : r + rows, :], wg[base + k])
                    up = dot(a0[r : r + rows, :], wu[base + k])
                    p[r : r + rows, pl.ds(pl.multiple_of((2 * i + k) * W, W), W)] = (gate * jax.nn.sigmoid(gate) * up).astype(BF16)
            return carry

        lax.fori_loop(0, per // 2, pair, 0)
        load_down.wait()
        for r in range(0, tokens, rows):
            made = dot(p[r : r + rows, :], down_all[...]).astype(BF16).astype(F32)
            out = (h[r : r + rows, :].astype(F32) + made).astype(BF16)
            h[r : r + rows, :] = out
            a1[r : r + rows, :] = normed(out)
        at_[...] = a1[...].T
        acc[...] = jnp.zeros_like(acc)
        load_dy.wait()
        dt[...] = d[...].T
        fetch_tile(jnp.int32(0), False)
        fetch_tile(jnp.int32(1), True)
        tile_forward(0, a1, d)

    def compute(tile):
        slot, after = rem(tile, 4), rem(tile + 1, 4)

        @pl.when(tile + 1 < tiles)
        def _():
            fetch_tile(tile + 1, False)

        @pl.when(tile + 2 < tiles)
        def _():
            fetch_tile(tile + 2, True)

        @pl.when(tile < per - 1)
        def _():
            tile_gradients(tile, dt)
            tile_by_input(slot)
            tile_forward(after, a1, d)

        @pl.when(tile == per - 1)
        def _():
            tile_by_input(slot)
            tile_gradients(tile, dt)
            through_norm()
            at_[...] = a0[...].T
            dt[...] = d[...].T
            tile_forward(after, a0, d)

        @pl.when((tile >= per) & (tile < tiles - 1))
        def _():
            tile_gradients(tile, dt)
            tile_forward(after, a0, d)

        @pl.when(tile == tiles - 1)
        def _():
            tile_gradients(tile, dt)


    def sem(array, color, stage, tile):
        return array.at[color, STAGES.index(stage), rem(tile, SLOTS)]

    def put(src, dst, color, stage, tile, where):
        pltpu.make_async_remote_copy(
            src_ref=src, dst_ref=dst, send_sem=sem(send, color, stage, tile), recv_sem=sem(recv, color, stage, tile),
            device_id=where, device_id_type=MESH,
        ).start()

    def wait(array, ref, color, stage, tile):
        pltpu.make_async_copy(ref, ref, sem(array, color, stage, tile)).wait()

    def some(tile, color, count):
        return g.at[tile, color, pl.ds(0, count), :]

    def part_at(color, tile, row, count):
        return g.at[tile, color, pl.ds(pl.multiple_of(row, 16), count), :]

    def ring_sum(color, tile, step):
        axis = plan.axes[color][0]
        n, chunk = sizes[axis], plan.chunk[color]
        slot, out, far = rem(tile, R_SLOTS), rem(tile, 2), n // 2 + 1 - step
        for direction in range(2 if step > 1 else 1):
            to = way if direction == 0 else -way
            lines = pl.ds(pl.multiple_of(along(axis, to * far) * chunk, 8), chunk)
            total = s[rem(tile, S_SLOTS), color, lines, :]
            if step > 1 + direction:
                total += ring_in[color][slot, step - 2, direction].astype(F32)
            ring_out[color][out, step - 1, direction] = total.astype(BF16)
            put(ring_out[color].at[out, step - 1, direction], ring_in[color].at[slot, step - 1, direction],
                color, f"r{step}", tile, device(axis, along(axis, to)))

    def ring_wait(color, tile, step):
        for array, buffer, slot in ((recv, ring_in[color], rem(tile, R_SLOTS)), (send, ring_out[color], rem(tile, 2))):
            wait(array, buffer.at[slot, step - 1] if step > 1 else buffer.at[slot, 0, 0], color, f"r{step}", tile)

    def ring_end(color, tile):
        axis = plan.axes[color][0]
        n, chunk = sizes[axis], plan.chunk[color]
        lines = pl.ds(pl.multiple_of(at[axis] * chunk, 8), chunk)
        total = s[rem(tile, S_SLOTS), color, lines, :]
        for direction in range(2 if n > 2 else 1):
            total += ring_in[color][rem(tile, R_SLOTS), n // 2 - 1, direction].astype(F32)
        return total

    def exchange(color, tile, index):
        axis, piece = plan.axes[color][1], plan.piece[color]
        for step in range(1, sizes[axis]):
            owner = along(axis, step)
            lines = pl.ds(pl.multiple_of(owner * piece, 8), piece)
            pair_out[color][rem(index, 2), step - 1] = kept[color][rem(index, 2), lines, :].astype(BF16)
            put(pair_out[color].at[rem(index, 2), step - 1], pair_in[color].at[rem(index, R_SLOTS), step - 1], color, "p2", tile, device(axis, owner))

    def exchanged(color, tile, index):
        axis, last, piece = plan.axes[color][1], plan.axes[color][2], plan.piece[color]
        wait(recv, pair_in[color].at[rem(index, R_SLOTS)], color, "p2", tile)
        wait(send, pair_out[color].at[rem(index, 2)], color, "p2", tile)
        lines = pl.ds(pl.multiple_of(at[axis] * piece, 8), piece)
        total = kept[color][rem(index, 2), lines, :]
        for step in range(1, sizes[axis]):
            total += pair_in[color][rem(index, R_SLOTS), step - 1].astype(F32)
        owner = rem(index, sizes[last])

        @pl.when(at[last] != owner)
        def _():
            own_out[color][rem(index, 4)] = total.astype(BF16)
            put(own_out[color].at[rem(index, 4)], own_in[color].at[div(index, sizes[last]), rem(at[last] - owner + sizes[last], sizes[last]) - 1],
                color, "p3", tile, device(last, owner))

        @pl.when(at[last] == owner)
        def _():
            own_kept[color][rem(index, 4)] = total

    def place(color, tile):
        first, second = plan.axes[color][:2]
        chunk, piece, q = plan.chunk[color], plan.piece[color], at[second]
        base = core * half + at[first] * chunk
        if color < 2:
            return tile, base + q * piece
        count = chunk // piece
        return tile - 1 + div(q, count), base + rem(q, count) * piece

    def own_step(color, tile, index):
        last, piece = plan.axes[color][2], plan.piece[color]
        n = sizes[last]
        owner = rem(index, n)

        @pl.when(at[last] == owner)
        def _():
            wait(recv, own_in[color].at[div(index, n)], color, "p3", tile)
            total = own_kept[color][rem(index, 4)]
            for step in range(1, n):
                total += own_in[color][div(index, n), step - 1].astype(F32)
            final = total.astype(BF16)
            where, row = place(color, tile)
            g[where, color, pl.ds(pl.multiple_of(row, 16), piece), :] = final
            for step in range(1, n):
                put(part_at(color, where, row, piece), part_at(color, where, row, piece), color, "b3", tile, device(last, along(last, step)))
            wide = final.astype(F32)
            mine_sq = sq.at[0, at[SQ_AXES[0]]]
            mine_sq[...] += jnp.sum((wide * wide).reshape(piece // 8, 8, LANES), axis=0)

        @pl.when(at[last] != owner)
        def _():
            wait(send, own_out[color].at[rem(index, 4)], color, "p3", tile)

    def spread(color, tile, index):
        second, last, piece = *plan.axes[color][1:], plan.piece[color]
        n = sizes[last]
        owner = rem(index, n)

        @pl.when(at[last] == owner)
        def _():
            wait(send, some(tile, color, (n - 1) * piece), color, "b3", tile)

        @pl.when(at[last] != owner)
        def _():
            wait(recv, some(tile, color, piece), color, "b3", tile)

        where, row = place(color, tile)
        for step in range(1, sizes[second]):
            put(part_at(color, where, row, piece), part_at(color, where, row, piece), color, "b2", tile, device(second, along(second, step)))

    def spread_wait(color, tile):
        count = (sizes[plan.axes[color][1]] - 1) * plan.piece[color]
        wait(recv, some(tile, color, count), color, "b2", tile)
        wait(send, some(tile, color, count), color, "b2", tile)

    def ring_gather(color, tile, step):
        axis, chunk = plan.axes[color][0], plan.chunk[color]
        n = sizes[axis]
        for direction in range(2 if step < n // 2 else 1):
            to = way if direction == 0 else -way
            row = core * half + along(axis, -to * (step - 1)) * chunk
            put(part_at(color, tile, row, chunk), part_at(color, tile, row, chunk), color, f"a{step}", tile, device(axis, along(axis, to)))

    def ring_gather_wait(color, tile, step):
        axis, chunk = plan.axes[color][0], plan.chunk[color]
        count = (2 if step < sizes[axis] // 2 else 1) * chunk
        wait(recv, some(tile, color, count), color, f"a{step}", tile)
        wait(send, some(tile, color, count), color, f"a{step}", tile)

    def core_gather(color, tile):
        put(part_at(color, tile, core * half, half), part_at(color, tile, core * half, half), color, "out", tile, device(other_core=True))

    def finish(color, tile):
        wait(recv, some(tile, color, half), color, "out", tile)
        wait(send, some(tile, color, half), color, "out", tile)
        pltpu.make_async_copy(g.at[tile, color], g_out.at[tile, color], out_sem.at[color, rem(tile, 2)]).start()

    def finished(color, tile):
        pltpu.make_async_copy(g.at[tile, color], g_out.at[tile, color], out_sem.at[color, rem(tile, 2)]).wait()

    def core_send(tile):
        put(mine.at[rem(tile, 2)], taken.at[rem(tile, 4)], 0, "core", tile, device(other_core=True))

    def core_take(tile):
        wait(recv, taken.at[rem(tile, 4)], 0, "core", tile)
        wait(send, taken.at[rem(tile, 4)], 0, "core", tile)
        for color in range(3):
            s[rem(tile, S_SLOTS), color] += taken[rem(tile, 4), color].astype(F32)
            ring_sum(color, tile, 1)

    def sq_peers(level):
        if level == 3:
            return [(core, device(other_core=True))]
        axis = SQ_AXES[level]
        return [(at[axis], device(axis, along(axis, step))) for step in range(1, sizes[axis])]

    def sq_send(level):
        for index, peer in sq_peers(level):
            pltpu.make_async_remote_copy(
                src_ref=sq.at[level, index], dst_ref=sq.at[level, index], send_sem=sq_send_sem.at[level], recv_sem=sq_recv.at[level],
                device_id=peer, device_id_type=MESH,
            ).start()

    def sq_take(level):
        count = len(sq_peers(level))
        for array in (sq_recv, sq_send_sem):
            ref = sq.at[level, pl.ds(0, count)]
            pltpu.make_async_copy(ref, ref, array.at[level]).wait()
        total = sq[level, 0]
        for i in range(1, count + 1):
            total += sq[level, i]
        if level == 3:
            squares[...] = total
        else:
            sq[level + 1, (at[SQ_AXES[level + 1]] if level < 2 else core)] = total
            sq_send(level + 1)

    rings = [sizes[a[0]] // 2 for a in plan.axes]

    def index_of(color, tile):
        return tile if color < 2 else div(tile, 2)

    def ring_next(color, step):
        def job(tile):
            ring_wait(color, tile, step - 1)
            ring_sum(color, tile, step)
        return job

    def ring_last(color):
        def job(tile):
            ring_wait(color, tile, rings[color])
            if color < 2:
                kept[color][rem(tile, 2)] = ring_end(color, tile)
                exchange(color, tile, tile)
            else:
                chunk = plan.chunk[color]
                kept[color][rem(div(tile, 2), 2), pl.ds(pl.multiple_of(rem(tile, 2) * chunk, 8), chunk), :] = ring_end(color, tile)
        return job

    ALL, ODD, FINAL = range(3)
    jobs = []
    for color in range(3):
        which = ODD if color == 2 else ALL
        for step in range(2, rings[color] + 1):
            jobs.append((step + 1, ALL, ring_next(color, step)))
        end = rings[color] + 2
        jobs.append((end, ALL, ring_last(color)))
        if color == 2:
            jobs.append((end, ODD, lambda tile: exchange(2, tile, div(tile, 2))))
        jobs.append((end + 1, which, lambda tile, c=color: exchanged(c, tile, index_of(c, tile))))
        jobs.append((end + 3, which, lambda tile, c=color: own_step(c, tile, index_of(c, tile))))
        jobs.append((end + 5, which, lambda tile, c=color: spread(c, tile, index_of(c, tile))))
        jobs.append((end + 6, which, lambda tile, c=color: spread_wait(c, tile)))
        begin = end + 6 + (1 if color == 2 else 0)
        for step in range(1, rings[color] + 1):
            def gather(tile, c=color, step=step):
                if step > 1:
                    ring_gather_wait(c, tile, step - 1)
                ring_gather(c, tile, step)
            jobs.append((begin + step - 1, ALL, gather))

        def gathered(tile, c=color):
            ring_gather_wait(c, tile, rings[c])
            core_gather(c, tile)
        jobs.append((begin + rings[color], ALL, gathered))
        jobs.append((begin + rings[color] + 1, ALL, lambda tile, c=color: finish(c, tile)))
        jobs.append((begin + rings[color] + 2, ALL, lambda tile, c=color: finished(c, tile)))
    summed = max(rings) + 2 + 3
    jobs.append((summed, FINAL, lambda tile: sq_send(0)))
    for level in range(4):
        jobs.append((summed + 1 + level, FINAL, lambda tile, level=level: sq_take(level)))
    jobs.sort(key=lambda job: job[0])
    ticks = tiles + jobs[-1][0]

    peers = [device(other_core=True)]
    for axis in range(3):
        peers += [device(axis, along(axis, step)) for step in range(1, sizes[axis])]
    barrier = pltpu.get_barrier_semaphore()
    for peer in peers:
        pl.semaphore_signal(barrier, inc=1, device_id=peer, device_id_type=MESH)
    sq[...] = jnp.zeros_like(sq)
    forward()
    pl.semaphore_wait(barrier, len(peers))

    def tick(now, carry):
        for delay, which, job in jobs:
            tile = now - delay
            there = (tile >= 0) & (tile < tiles) if which != FINAL else tile == tiles - 1
            if which == ODD:
                there &= rem(tile, 2) == 1
            pl.when(there)(functools.partial(job, tile))

        @pl.when(now < tiles)
        def _():
            compute(now)
            core_send(now)

        @pl.when((now >= 1) & (now <= tiles))
        def _():
            core_take(now - 1)
        return carry

    lax.fori_loop(0, ticks, tick, 0)


S_SLOTS, R_SLOTS = 6, 4
SQ_AXES = (2, 1, 0)


def gradients(plan, x, dy, weights):
    sizes, tiles, half, chunk, piece = plan.sizes, plan.tiles, plan.half, plan.chunk, plan.piece
    n1, n2, n3 = ([sizes[a[i]] for a in plan.axes] for i in range(3))
    owned = [-(-(tiles if c < 2 else tiles // 2) // n3[c]) for c in range(3)]
    tokens, width = x.shape[1:]
    hidden = tiles // 2 * W
    vmem, dma = pltpu.VMEM, pltpu.SemaphoreType.DMA
    scratch = [
        vmem((tiles, 3, 2 * half, LANES), BF16),
        vmem((2, 3, half, LANES), BF16),
        vmem((4, 3, half, LANES), BF16),
        vmem((S_SLOTS, 3, half, LANES), F32),
    ]
    scratch += [vmem((R_SLOTS, n1[c] // 2, 2, chunk[c], LANES), BF16) for c in range(3)]
    scratch += [vmem((2, n1[c] // 2, 2, chunk[c], LANES), BF16) for c in range(3)]
    scratch += [vmem((R_SLOTS, n2[c] - 1, piece[c], LANES), BF16) for c in range(3)]
    scratch += [vmem((2, n2[c] - 1, piece[c], LANES), BF16) for c in range(3)]
    scratch += [vmem((2, n2[c] * piece[c], LANES), F32) for c in range(3)]
    scratch += [vmem((owned[c], n3[c] - 1, piece[c], LANES), BF16) for c in range(3)]
    scratch += [vmem((4, piece[c], LANES), BF16) for c in range(3)]
    scratch += [vmem((4, piece[c], LANES), F32) for c in range(3)]
    scratch += [vmem((4, 8, 8, LANES), F32)]
    scratch += [dma((3, len(STAGES), SLOTS)), dma((3, len(STAGES), SLOTS)), dma((3, 2)), dma((4,)), dma((4,))]
    state, turned = vmem((tokens, width), BF16), vmem((width, tokens), BF16)
    scratch += [state, state, state, state, turned, turned, vmem((tokens, width), F32)]
    scratch += [vmem((tokens, hidden), BF16), vmem((tokens, W), BF16), vmem((tokens, W), BF16), vmem((hidden, width), BF16)]
    scratch += [vmem((4, width, W), BF16), vmem((4, width, W), BF16), vmem((4, W, width), BF16), dma((3,)), dma((4, 3))]
    flops = 34 * tokens * width * hidden
    return pl.pallas_call(
        functools.partial(train_kernel, plan),
        name="gradients",
        out_shape=(jax.ShapeDtypeStruct((tiles, 3, 2 * half, LANES), BF16), jax.ShapeDtypeStruct((8, LANES), F32)),
        in_specs=[pl.BlockSpec(memory_space=pl.ANY)] * 5,
        out_specs=(pl.BlockSpec(memory_space=pl.ANY), pl.BlockSpec(memory_space=pltpu.VMEM)),
        scratch_shapes=scratch,
        cost_estimate=pl.CostEstimate(flops=flops, bytes_accessed=12 * width * hidden * 2, transcendentals=0),
        compiler_params=pltpu.CompilerParams(collective_id=0, has_side_effects=True, vmem_limit_bytes=67_000_000),
    )(x, dy, *weights)


def adamw_kernel(count, squares_ref, *refs):
    gs, ws, ms, vs, new_ws, new_ms, new_vs = (refs[i : i + 3] for i in range(0, 21, 3))
    factor = jnp.minimum(1.0, 0.5 * lax.rsqrt(jnp.sum(squares_ref[...]) / count + 1e-30))

    def update(color, g, rows, columns):
        g = g.astype(F32) * factor
        m = 0.9 * ms[color][0, rows, columns] + 0.1 * g
        v = 0.95 * vs[color][0, rows, columns] + 0.05 * g * g
        w = ws[color][0, rows, columns].astype(F32)
        new_ws[color][0, rows, columns] = (w - 0.02 * (m * lax.rsqrt(v + 1e-8) + 0.1 * w)).astype(BF16)
        new_ms[color][0, rows, columns] = m
        new_vs[color][0, rows, columns] = v

    for color in range(2):
        for t in range(gs[color].shape[0]):
            for block in range(2):
                update(color, gs[color][t, 0, block], slice(None), pl.ds((2 * t + block) * LANES, LANES))
    for block in range(2):
        update(2, gs[2][0, 0, block].astype(F32).T, pl.ds(block * LANES, LANES), slice(None))


def adamw(g, squares, weights, m, v):
    tiles, _, half = g.shape[0], 0, g.shape[2] // 2
    per = tiles // 2
    g = g.reshape(tiles, 3, 2, half, LANES)
    lines = half // per
    up = pl.BlockSpec((1, lines, W * per), lambda i: (1 - i // per, i % per, 0))
    down = pl.BlockSpec((1, W, half), lambda i: (1 - i // per, i % per, 0))
    three = [up, up, down]
    by = [pl.BlockSpec((per, 1, 2, lines, LANES), lambda i, c=c: (i // per, c, 0, i % per, 0)) for c in range(2)]
    by.append(pl.BlockSpec((1, 1, 2, half, LANES), lambda i: (i, 2, 0, 0, 0)))
    out = [jax.ShapeDtypeStruct(a.shape, a.dtype) for a in (*weights, *m, *v)]
    return pl.pallas_call(
        functools.partial(adamw_kernel, float(sum(w.size for w in weights))),
        name="adamw",
        grid=(tiles,),
        out_shape=out,
        in_specs=[pl.BlockSpec(squares.shape, lambda i: (0, 0))] + by + three * 3,
        out_specs=three * 3,
        compiler_params=pltpu.CompilerParams(vmem_limit_bytes=62_000_000),
    )(squares, g, g, g, *weights, *m, *v)


def solution(mesh):
    plan = Plan((4, 4, 8), 16, 768)

    def step(x, dy, *arrays):
        weights, m, v = (arrays[i : i + 3] for i in (0, 3, 6))
        g, squares = gradients(plan, x, dy, weights)
        return tuple(adamw(g, squares, weights, m, v))

    return jax.shard_map(
        step,
        mesh=mesh,
        in_specs=(P(("rep", "dp"), None, None),) * 2 + (P(None, None, None),) * 9,
        out_specs=(P("rep", None, None),) * 9,
        check_vma=False,
    )
```

profile of v0, /device:TPU:1, one launch (start us, length us, event | category | flops | bytes accessed | tf_op | source)
XLA Modules:
  0.0 238.9 jit_solution(12605109784458505791)
XLA Ops:
  0.6 171.8 %gradients.1 = (bf16[16,3,1536,128]{3,2,1,0:T(8,128)(2,1)}, f32[8,128]{1,0:T(8,128)}) custom-call(bf16[1,1024,768]{2,1,0:T(8,128)(2,1)} %refs_0_.1, bf16[1,1024,768]{2,1,0:T(8,128)(2,1)} %refs_1_.1, bf16[2,768,2048]{2,1,0:T(8,128)(2,1)} %refs_3_.3, bf16[2,768,2048]{2,1,0:T(8,128)(2,1)} %refs_4_.3, bf16[2,2048,768]{2,1,0:T(8,128)(2,1)} %refs_5_.1), custom_call_target="tpu_custom_call" | custom-call | flops 54760833024 | bytes 37748736 | tf_op jit(solution)/shard_map/gradients/pallas_call | solution.py:526
  172.4 66.3 %adamw.1 = (bf16[2,768,2048]{2,1,0:T(8,128)(2,1)}, bf16[2,768,2048]{2,1,0:T(8,128)(2,1)}, bf16[2,2048,768]{2,1,0:T(8,128)(2,1)}, f32[2,768,2048]{2,1,0:T(8,128)}...) custom-call(f32[8,128]{1,0:T(8,128)} %get-tuple-element.11.squares_r, ...), custom_call_target="tpu_custom_call" | custom-call | tf_op jit(solution)/shard_map/adamw/pallas_call | solution.py:570
where the time goes:
time: 239 us
  Pallas kernels  238 us (100%)
    pallas_call x1, Pallas kernels, gradients(): pl.pallas_call(functools.partial(train_kernel, plan), name='gradients', o...  172 us
    pallas_call x1, Pallas kernels, adamw(): pl.pallas_call(functools.partial(adamw_kernel, float(sum((w.size for w in...  66.3 us

commit v1 on v0

v1 whole, which is shorter than its diff:
```python
import functools

import jax
import jax.numpy as jnp
from jax import lax
from jax.experimental import pallas as pl
from jax.experimental.pallas import tpu as pltpu
from jax.sharding import PartitionSpec as P

F32, BF16 = jnp.float32, jnp.bfloat16
MESH = pl.DeviceIdType.MESH
SLOTS = 4
W = 256
LANES = 128


def ring_steps(n):
    half = n // 2
    sums = [[(1, half + 1 - k, 0 if k > 1 else None)] + ([(-1, k - half - 1, 1 if k > 2 else None)] if k > 1 else []) for k in range(1, half + 1)]
    copies = [[(1, 1 - k)] + ([(-1, k - 1)] if k < half else []) for k in range(1, half + 1)]
    return sums, copies


class Plan:
    def __init__(self, sizes, tiles, half):
        self.sizes, self.tiles, self.half = sizes, tiles, half
        groups = [((0, (0, 1, 2)), (1, (1, 0, 2))), ((2, (2, 0, 1)),)]
        self.members, self.span, self.sums, self.copies = [], [], [], []
        self.length, self.chunk, self.piece, self.owners, self.keys = [], [], [], [], [(0, "core")]
        for members in groups:
            n1, n2, n3 = (sizes[a] for a in members[0][1])
            assert all(tuple(sizes[a] for a in axes) == (n1, n2, n3) for _, axes in members)
            sums, copies = ring_steps(n1)
            self.members.append(members)
            self.span.append((0, tiles))
            self.sums.append(sums)
            self.copies.append(copies)
            self.length.append((n1, n2, n3))
            self.chunk.append(half // n1)
            self.piece.append(half // (n1 * n2))
            self.owners.append(half // (n1 * n2) // 8)
            self.keys += [(len(self.span) - 1, f"{c}{k + 1}") for c in "ra" for k in range(len(sums))]
            self.keys += [(len(self.span) - 1, name) for name in ("p2", "p3", "b3", "b2", "out")]


def rem(a, b):
    return lax.rem(a, jnp.int32(b))


def div(a, b):
    return lax.div(a, jnp.int32(b))


def dot(a, b, dims=((1,), (0,))):
    return lax.dot_general(a, b, (dims, ((), ())), preferred_element_type=F32)


LAST = ((1,), (1,))


def normed(h):
    wide = h.astype(F32)
    return (wide * lax.rsqrt(jnp.mean(wide * wide, -1, keepdims=True) + 1e-6)).astype(BF16)


def train_kernel(plan, *refs):
    sizes, tiles, half = plan.sizes, plan.tiles, plan.half
    x_hbm, dy_hbm, gate_hbm, up_hbm, down_hbm = refs[:5]
    g, squares = refs[5:7]
    scratch = list(refs[7:])

    def take(count):
        out, scratch[:] = scratch[:count], scratch[count:]
        return out

    mine, taken, s = take(3)
    ring_in, ring_out, pair_in, pair_out, kept, own_in, own_out, own_kept = (take(len(plan.span)) for _ in range(8))
    sq, = take(1)
    recv, send, sq_recv, sq_send_sem = take(4)
    h, d, a0, a1, at_, dt, acc, p, dg, du, down_all, wg, wu, wd, in_sem, w_sem = take(16)
    tokens, width = h.shape
    per = tiles // 2
    rows = min(256, tokens)

    me = lax.axis_index("dp")
    core = rem(me, 2)
    at = [div(me, 2 * sizes[1] * sizes[2]), rem(div(me, 2 * sizes[2]), sizes[1]), rem(div(me, 2), sizes[2])]
    way = 1 - 2 * core

    def device(axis=None, place=None, other_core=False):
        c = [place if a == axis else at[a] for a in range(3)]
        return {"dp": ((c[0] * sizes[1] + c[1]) * sizes[2] + c[2]) * 2 + ((1 - core) if other_core else core)}

    def along(axis, step):
        return rem(at[axis] + step + 2 * sizes[axis], sizes[axis])


    def fetch(layer, t, slot, start, down=True):
        cols = pl.ds(pl.multiple_of(t * W, W), W)
        copies = [(gate_hbm.at[layer, :, cols], wg.at[slot]), (up_hbm.at[layer, :, cols], wu.at[slot])]
        if down:
            copies.append((down_hbm.at[layer, cols, :], wd.at[slot]))
        for i, (src, dst) in enumerate(copies):
            copy = pltpu.make_async_copy(src, dst, w_sem.at[slot, i])
            copy.start() if start else copy.wait()

    def fetch_tile(q, start):
        for layer in range(2):
            first = (1 - layer) * per

            @pl.when((q >= first) & (q < first + per))
            def _():
                fetch(layer, q - first, rem(q, 4), start)

    def tile_forward(slot, a, d):
        for r in range(0, tokens, rows):
            block = pl.ds(r, rows)
            gate = dot(a[block, :], wg[slot])
            up = dot(a[block, :], wu[slot])
            by_p = dot(d[block, :], wd[slot], LAST).astype(BF16).astype(F32)
            sig = jax.nn.sigmoid(gate)
            act = gate * sig
            p[block, 0:W] = (act * up).astype(BF16)
            du[block, :] = (by_p * act).astype(BF16)
            dg[block, :] = (by_p * up * (sig * (1 + gate * (1 - sig)))).astype(BF16)

    def tile_gradients(tile, dt):
        for color, (left, right) in enumerate(((at_, dg), (at_, du), (dt, p))):
            out = dot(left[...], right[:, 0:W])
            low, high = out[:, :LANES], out[:, LANES:]
            s[rem(tile, S_SLOTS), color] = jnp.where(core == 0, low, high)
            mine[rem(tile, 2), color] = jnp.where(core == 0, high, low).astype(BF16)

    def tile_by_input(slot):
        for r in range(0, tokens, rows):
            block = pl.ds(r, rows)
            acc[block, :] += dot(dg[block, :], wg[slot], LAST) + dot(du[block, :], wu[slot], LAST)

    def through_norm():
        for r in range(0, tokens, rows):
            block = pl.ds(r, rows)
            wide = h[block, :].astype(F32)
            scale = lax.rsqrt(jnp.mean(wide * wide, -1, keepdims=True) + 1e-6)
            by_a = acc[block, :].astype(BF16).astype(F32)
            by_h = by_a * scale - wide * (scale * scale * scale * (jnp.sum(by_a * wide, -1, keepdims=True) * (1.0 / width)))
            d[block, :] = (d[block, :].astype(F32) + by_h.astype(BF16).astype(F32)).astype(BF16)

    def forward():
        load_x = pltpu.make_async_copy(x_hbm.at[0], h, in_sem.at[0])
        load_dy = pltpu.make_async_copy(dy_hbm.at[0], d, in_sem.at[1])
        load_down = pltpu.make_async_copy(down_hbm.at[0], down_all, in_sem.at[2])
        load_x.start()
        for t in range(2):
            fetch(0, t, t, True, False)
        load_down.start()
        load_dy.start()
        load_x.wait()
        for r in range(0, tokens, rows):
            a0[r : r + rows, :] = normed(h[r : r + rows, :])

        def pair(i, carry):
            base = 2 * rem(i, 2)
            for k in range(2):
                fetch(0, 2 * i + k, base + k, False, False)

            @pl.when(i + 1 < per // 2)
            def _():
                for k in range(2):
                    fetch(0, 2 * i + 2 + k, 2 - base + k, True, False)

            @pl.when(i + 1 == per // 2)
            def _():
                fetch(1, 0, 2 - base, True)

            for k in range(2):
                for r in range(0, tokens, rows):
                    gate = dot(a0[r : r + rows, :], wg[base + k])
                    up = dot(a0[r : r + rows, :], wu[base + k])
                    p[r : r + rows, pl.ds(pl.multiple_of((2 * i + k) * W, W), W)] = (gate * jax.nn.sigmoid(gate) * up).astype(BF16)
            return carry

        lax.fori_loop(0, per // 2, pair, 0)
        load_down.wait()
        for r in range(0, tokens, rows):
            made = dot(p[r : r + rows, :], down_all[...]).astype(BF16).astype(F32)
            out = (h[r : r + rows, :].astype(F32) + made).astype(BF16)
            h[r : r + rows, :] = out
            a1[r : r + rows, :] = normed(out)
        at_[...] = a1[...].T
        acc[...] = jnp.zeros_like(acc)
        load_dy.wait()
        dt[...] = d[...].T
        fetch_tile(jnp.int32(0), False)
        fetch_tile(jnp.int32(1), True)
        tile_forward(0, a1, d)

    def gradients_of(tile):
        tile_gradients(tile, dt)

    def rest(tile):
        slot, after = rem(tile, 4), rem(tile + 1, 4)

        @pl.when(tile + 1 < tiles)
        def _():
            fetch_tile(tile + 1, False)

        @pl.when(tile + 2 < tiles)
        def _():
            fetch_tile(tile + 2, True)

        @pl.when(tile < per - 1)
        def _():
            tile_by_input(slot)
            tile_forward(after, a1, d)

        @pl.when(tile == per - 1)
        def _():
            tile_by_input(slot)
            through_norm()
            at_[...] = a0[...].T
            dt[...] = d[...].T
            tile_forward(after, a0, d)

        @pl.when((tile >= per) & (tile < tiles - 1))
        def _():
            tile_forward(after, a0, d)


    def sem(array, group, stage, tile):
        return array.at[plan.keys.index((group, stage)), rem(tile, SLOTS)]

    def put(src, dst, group, stage, tile, where):
        pltpu.make_async_remote_copy(
            src_ref=src, dst_ref=dst, send_sem=sem(send, group, stage, tile), recv_sem=sem(recv, group, stage, tile),
            device_id=where, device_id_type=MESH,
        ).start()

    def wait(array, ref, group, stage, tile):
        pltpu.make_async_copy(ref, ref, sem(array, group, stage, tile)).wait()

    def some(group, tile, count):
        return g.at[tile, plan.members[group][0][0], pl.ds(0, count * len(plan.members[group])), :]

    def spot(weight, tile, row, count):
        return g.at[tile, weight, pl.ds(pl.multiple_of(row, 8), count), :]

    def eight(row, count):
        return pl.ds(pl.multiple_of(row, 8), count)

    def first_sends(group, tile, step):
        slot, out, chunk = rem(tile, R_SLOTS), rem(tile, 2), plan.chunk[group]
        for m, (weight, axes) in enumerate(plan.members[group]):
            for i, (to, whose, before) in enumerate(plan.sums[group][step - 1]):
                total = s[rem(tile, S_SLOTS), weight, eight(along(axes[0], way * whose) * chunk, chunk), :]
                if before is not None:
                    total += ring_in[group][slot, step - 2, before, m].astype(F32)
                ring_out[group][out, step - 1, i, m] = total.astype(BF16)
                put(ring_out[group].at[out, step - 1, i, m], ring_in[group].at[slot, step - 1, i, m], group, f"r{step}", tile,
                    device(axes[0], along(axes[0], way * to)))

    def first_wait(group, tile, step):
        count = len(plan.sums[group][step - 1])
        wait(recv, ring_in[group].at[rem(tile, R_SLOTS), step - 1, pl.ds(0, count)], group, f"r{step}", tile)
        wait(send, ring_out[group].at[rem(tile, 2), step - 1, pl.ds(0, count)], group, f"r{step}", tile)

    def first_next(group, tile, step):
        first_wait(group, tile, step - 1)
        first_sends(group, tile, step)

    def first_last(group, tile):
        steps, chunk, piece, slot = len(plan.sums[group]), plan.chunk[group], plan.piece[group], rem(tile, 2)
        first_wait(group, tile, steps)
        for m, (weight, axes) in enumerate(plan.members[group]):
            total = s[rem(tile, S_SLOTS), weight, eight(at[axes[0]] * chunk, chunk), :]
            for i in range(len(plan.sums[group][-1])):
                total += ring_in[group][rem(tile, R_SLOTS), steps - 1, i, m].astype(F32)
            kept[group][slot, m] = total
            for k in range(1, sizes[axes[1]]):
                owner = along(axes[1], k)
                pair_out[group][slot, k - 1, m] = kept[group][slot, m, eight(owner * piece, piece), :].astype(BF16)
                put(pair_out[group].at[slot, k - 1, m], pair_in[group].at[rem(tile, R_SLOTS), k - 1, m], group, "p2", tile, device(axes[1], owner))

    def exchanged(group, tile):
        piece, slot, n = plan.piece[group], rem(tile, 4), plan.length[group][2]
        wait(recv, pair_in[group].at[rem(tile, R_SLOTS)], group, "p2", tile)
        wait(send, pair_out[group].at[rem(tile, 2)], group, "p2", tile)
        for m, (weight, axes) in enumerate(plan.members[group]):
            total = kept[group][rem(tile, 2), m, eight(at[axes[1]] * piece, piece), :]
            for k in range(1, sizes[axes[1]]):
                total += pair_in[group][rem(tile, R_SLOTS), k - 1, m].astype(F32)
            own_kept[group][slot, m] = total
            own_out[group][slot, m] = total.astype(BF16)
        last = plan.members[group][0][1][2]
        for owner in range(plan.owners[group]):

            @pl.when(at[last] != owner)
            def _():
                put(own_out[group].at[slot, :, pl.ds(8 * owner, 8)], own_in[group].at[slot, rem(at[last] + (n - 1 - owner), n)],
                    group, "p3", tile, device(last, jnp.int32(owner)))

    def place(group, axes):
        return core * half + at[axes[0]] * plan.chunk[group] + at[axes[1]] * plan.piece[group]

    def own_step(group, tile):
        n, slot, last = plan.length[group][2], rem(tile, 4), plan.members[group][0][1][2]

        @pl.when(at[last] < plan.owners[group])
        def _():
            wait(recv, own_in[group].at[slot], group, "p3", tile)
            for m, (weight, axes) in enumerate(plan.members[group]):
                total = own_kept[group][slot, m, eight(8 * at[last], 8), :]
                for k in range(1, n):
                    total += own_in[group][slot, k - 1, m].astype(F32)
                final = total.astype(BF16)
                row = place(group, axes) + 8 * at[last]
                g[tile, weight, eight(row, 8), :] = final
                for k in range(1, n):
                    put(spot(weight, tile, row, 8), spot(weight, tile, row, 8), group, "b3", tile, device(last, along(last, k)))
                wide = final.astype(F32)
                mine_sq = sq.at[0, at[SQ_AXES[0]]]
                mine_sq[...] += wide * wide

        line_wait(send, group, tile, "p3")

    def line_wait(array, group, tile, stage):
        owners, last = plan.owners[group], plan.members[group][0][1][2]
        if owners > 1:

            @pl.when(at[last] < owners)
            def _():
                wait(array, some(group, tile, 8 * (owners - 1)), group, stage, tile)

        if owners < sizes[last]:

            @pl.when(at[last] >= owners)
            def _():
                wait(array, some(group, tile, 8 * owners), group, stage, tile)

    def spread(group, tile):
        last, piece = plan.members[group][0][1][2], plan.piece[group]

        @pl.when(at[last] < plan.owners[group])
        def _():
            wait(send, some(group, tile, (plan.length[group][2] - 1) * 8), group, "b3", tile)

        line_wait(recv, group, tile, "b3")
        for weight, axes in plan.members[group]:
            row = place(group, axes)
            for k in range(1, sizes[axes[1]]):
                put(spot(weight, tile, row, piece), spot(weight, tile, row, piece), group, "b2", tile, device(axes[1], along(axes[1], k)))

    def gather(group, tile, step):
        chunk = plan.chunk[group]
        if step == 1:
            for array in (recv, send):
                wait(array, some(group, tile, (plan.length[group][1] - 1) * plan.piece[group]), group, "b2", tile)
        else:
            gather_wait(group, tile, step - 1)
        for weight, axes in plan.members[group]:
            for to, whose in plan.copies[group][step - 1]:
                row = core * half + along(axes[0], way * whose) * chunk
                put(spot(weight, tile, row, chunk), spot(weight, tile, row, chunk), group, f"a{step}", tile, device(axes[0], along(axes[0], way * to)))

    def gather_wait(group, tile, step):
        for array in (recv, send):
            wait(array, some(group, tile, len(plan.copies[group][step - 1]) * plan.chunk[group]), group, f"a{step}", tile)

    def both(group):
        weights = [weight for weight, _ in plan.members[group]]
        return pl.ds(weights[0], len(weights))

    def gathered(group, tile):
        gather_wait(group, tile, len(plan.copies[group]))
        mine_half = g.at[tile, both(group), eight(core * half, half), :]
        put(mine_half, mine_half, group, "out", tile, device(other_core=True))

    def finish(group, tile):
        for array in (recv, send):
            wait(array, some(group, tile, half), group, "out", tile)

    def core_send(tile):
        put(mine.at[rem(tile, 2)], taken.at[rem(tile, 2)], 0, "core", tile, device(other_core=True))

    def core_take(tile):
        wait(recv, taken.at[rem(tile, 2)], 0, "core", tile)
        wait(send, taken.at[rem(tile, 2)], 0, "core", tile)
        for weight in range(3):
            s[rem(tile, S_SLOTS), weight] += taken[rem(tile, 2), weight].astype(F32)

    def sq_peers(level):
        if level == 3:
            return [(core, device(other_core=True))]
        axis = SQ_AXES[level]
        return [(at[axis], device(axis, along(axis, step))) for step in range(1, sizes[axis])]

    def sq_send(level):
        for index, peer in sq_peers(level):
            pltpu.make_async_remote_copy(
                src_ref=sq.at[level, index], dst_ref=sq.at[level, index], send_sem=sq_send_sem.at[level], recv_sem=sq_recv.at[level],
                device_id=peer, device_id_type=MESH,
            ).start()

    def sq_take(level):
        count = len(sq_peers(level))
        for array in (sq_recv, sq_send_sem):
            ref = sq.at[level, pl.ds(0, count)]
            pltpu.make_async_copy(ref, ref, array.at[level]).wait()
        total = sq[level, 0]
        for i in range(1, count + 1):
            total += sq[level, i]
        if level == 3:
            squares[...] = total
        else:
            sq[level + 1, (at[SQ_AXES[level + 1]] if level < 2 else core)] = total
            sq_send(level + 1)

    jobs = [(1, 0, 0, tiles, core_take)]
    for group in range(len(plan.span)):
        def add(delay, part, job, *rest, group=group):
            jobs.append((delay, part, *plan.span[group], lambda tile: job(group, tile, *rest)))

        steps = len(plan.sums[group])
        add(1, 0, first_sends, 1)
        for step in range(2, steps + 1):
            add(step, 0, first_next, step)
        add(steps + 1, 0, first_last)
        add(steps + 2, 0, exchanged)
        own = steps + (4 if plan.length[group][2] > 4 else 3)
        add(own, 0, own_step)
        add(own + 1, 1, spread)
        for step in range(1, steps + 1):
            add(own + 1 + step, 1, gather, step)
        add(own + 2 + steps, 1, gathered)
        add(own + 3 + steps, 1, finish)
    summed = max(job[0] + job[3] - tiles for job in jobs if job[1] == 0)
    jobs.append((summed, 0, tiles - 1, tiles, lambda tile: sq_send(0)))
    for level in range(4):
        jobs.append((summed + 1 + level, 1, tiles - 1, tiles, lambda tile, level=level: sq_take(level)))
    jobs.sort(key=lambda job: job[0])
    ticks = max(job[0] + job[3] for job in jobs)

    peers = [device(other_core=True)]
    for axis in range(3):
        peers += [device(axis, along(axis, step)) for step in range(1, sizes[axis])]
    barrier = pltpu.get_barrier_semaphore()
    for peer in peers:
        pl.semaphore_signal(barrier, inc=1, device_id=peer, device_id_type=MESH)
    sq[...] = jnp.zeros_like(sq)
    forward()
    pl.semaphore_wait(barrier, len(peers))

    def run(now, some_jobs):
        for delay, _, first, end, job in some_jobs:
            tile = now - delay
            pl.when((tile >= first) & (tile < end))(functools.partial(job, tile))

    def tick(now, carry):
        for part in range(2):
            here = [job for job in jobs if job[1] == part]
            pl.when(now >= min(job[0] + job[2] for job in here))(functools.partial(run, now, here))

            @pl.when(now < tiles)
            def _():
                if part:
                    rest(now)
                else:
                    gradients_of(now)
                    core_send(now)
        return carry

    lax.fori_loop(0, ticks, tick, 0)


S_SLOTS, R_SLOTS = 5, 4
SQ_AXES = (2, 1, 0)


def gradients(plan, x, dy, weights):
    tiles, half, chunk, piece = plan.tiles, plan.half, plan.chunk, plan.piece
    tokens, width = x.shape[1:]
    hidden = tiles // 2 * W
    vmem, dma = pltpu.VMEM, pltpu.SemaphoreType.DMA
    scratch = [
        vmem((2, 3, half, LANES), BF16),
        vmem((2, 3, half, LANES), BF16),
        vmem((S_SLOTS, 3, half, LANES), F32),
    ]
    groups = range(len(plan.span))
    count = [len(members) for members in plan.members]
    most = [max(len(step) for step in sums) for sums in plan.sums]
    scratch += [vmem((R_SLOTS, len(plan.sums[c]), most[c], count[c], chunk[c], LANES), BF16) for c in groups]
    scratch += [vmem((2, len(plan.sums[c]), most[c], count[c], chunk[c], LANES), BF16) for c in groups]
    scratch += [vmem((R_SLOTS, plan.length[c][1] - 1, count[c], piece[c], LANES), BF16) for c in groups]
    scratch += [vmem((2, plan.length[c][1] - 1, count[c], piece[c], LANES), BF16) for c in groups]
    scratch += [vmem((2, count[c], chunk[c], LANES), F32) for c in groups]
    scratch += [vmem((4, plan.length[c][2] - 1, count[c], 8, LANES), BF16) for c in groups]
    scratch += [vmem((4, count[c], piece[c], LANES), BF16) for c in groups]
    scratch += [vmem((4, count[c], piece[c], LANES), F32) for c in groups]
    scratch += [vmem((4, 8, 8, LANES), F32)]
    scratch += [dma((len(plan.keys), SLOTS)), dma((len(plan.keys), SLOTS)), dma((4,)), dma((4,))]
    state, turned = vmem((tokens, width), BF16), vmem((width, tokens), BF16)
    scratch += [state, state, state, state, turned, turned, vmem((tokens, width), F32)]
    scratch += [vmem((tokens, hidden), BF16), vmem((tokens, W), BF16), vmem((tokens, W), BF16), vmem((hidden, width), BF16)]
    scratch += [vmem((4, width, W), BF16), vmem((4, width, W), BF16), vmem((4, W, width), BF16), dma((3,)), dma((4, 3))]
    flops = 34 * tokens * width * hidden
    return pl.pallas_call(
        functools.partial(train_kernel, plan),
        name="gradients",
        out_shape=(pltpu.VMEM((tiles, 3, 2 * half, LANES), BF16), jax.ShapeDtypeStruct((8, LANES), F32)),
        in_specs=[pl.BlockSpec(memory_space=pl.ANY)] * 5,
        out_specs=(pl.BlockSpec(memory_space=pltpu.VMEM), pl.BlockSpec(memory_space=pltpu.VMEM)),
        scratch_shapes=scratch,
        cost_estimate=pl.CostEstimate(flops=flops, bytes_accessed=12 * width * hidden * 2, transcendentals=0),
        compiler_params=pltpu.CompilerParams(collective_id=0, has_side_effects=True, vmem_limit_bytes=48_000_000),
    )(x, dy, *weights)


def adamw_kernel(count, squares_ref, g_ref, *refs):
    ws, ms, vs, new_ws, new_ms, new_vs = (refs[i : i + 3] for i in range(0, 18, 3))
    factor = jnp.minimum(1.0, 0.5 * lax.rsqrt(jnp.sum(squares_ref[...]) / count + 1e-30))
    step = pl.program_id(0)
    per, half, lines = g_ref.shape[0] // 2, g_ref.shape[2] // 2, ms[0].shape[1]
    first, at = div(step, per) * per, rem(step, per)

    def update(color, g, rows, columns):
        g = g.astype(F32) * factor
        m = 0.9 * ms[color][0, rows, columns] + 0.1 * g
        v = 0.95 * vs[color][0, rows, columns] + 0.05 * g * g
        w = ws[color][0, rows, columns].astype(F32)
        new_ws[color][0, rows, columns] = (w - 0.02 * (m * lax.rsqrt(v + 1e-8) + 0.1 * w)).astype(BF16)
        new_ms[color][0, rows, columns] = m
        new_vs[color][0, rows, columns] = v

    for color in range(2):
        for t in range(per):
            for block in range(2):
                g = g_ref[first + t, color, pl.ds(pl.multiple_of(block * half + at * lines, 8), lines), :]
                update(color, g, slice(None), pl.ds((2 * t + block) * LANES, LANES))
    for block in range(2):
        update(2, g_ref[step, 2, pl.ds(block * half, half), :].astype(F32).T, pl.ds(block * LANES, LANES), slice(None))


def adamw(g, squares, weights, m, v):
    tiles, half = g.shape[0], g.shape[2] // 2
    per = tiles // 2
    up = pl.BlockSpec((1, half // per, W * per), lambda i: (1 - i // per, i % per, 0))
    down = pl.BlockSpec((1, W, half), lambda i: (1 - i // per, i % per, 0))
    three = [up, up, down]
    out = [jax.ShapeDtypeStruct(a.shape, a.dtype) for a in (*weights, *m, *v)]
    return pl.pallas_call(
        functools.partial(adamw_kernel, float(sum(w.size for w in weights))),
        name="adamw",
        grid=(tiles,),
        out_shape=out,
        in_specs=[pl.BlockSpec(squares.shape, lambda i: (0, 0)), pl.BlockSpec(memory_space=pltpu.VMEM)] + three * 3,
        out_specs=three * 3,
        compiler_params=pltpu.CompilerParams(vmem_limit_bytes=48_000_000),
    )(squares, pltpu.with_memory_space_constraint(g, pltpu.VMEM), *weights, *m, *v)


def solution(mesh):
    plan = Plan((4, 4, 8), 16, 768)

    def step(x, dy, *arrays):
        weights, m, v = (arrays[i : i + 3] for i in (0, 3, 6))
        g, squares = gradients(plan, x, dy, weights)
        return tuple(adamw(g, squares, weights, m, v))

    return jax.shard_map(
        step,
        mesh=mesh,
        in_specs=(P(("rep", "dp"), None, None),) * 2 + (P(None, None, None),) * 9,
        out_specs=(P("rep", None, None),) * 9,
        check_vma=False,
    )
```

time: 239 us -> 213 us (0.89)
  Pallas kernels: 238 us -> 212 us
    pallas_call x1, Pallas kernels: 172 us -> 151 us  [gradients(): pl.pallas_call(functools.partial(train_kernel, plan), name='gradients', o...]
    pallas_call x1, Pallas kernels: 66.3 us -> 60.9 us  [adamw(): pl.pallas_call(functools.partial(adamw_kernel, float(sum((w.size for w in...]
where the time goes in v1:
time: 213 us
  Pallas kernels  212 us (100%)
    pallas_call x1, Pallas kernels, gradients(): pl.pallas_call(functools.partial(train_kernel, plan), name='gradients', o...  151 us
    pallas_call x1, Pallas kernels, adamw(): pl.pallas_call(functools.partial(adamw_kernel, float(sum((w.size for w in...  60.9 us

profile of v1, /device:TPU:1, one launch (start us, length us, event | category | flops | bytes accessed | tf_op | source)
XLA Modules:
  0.0 212.8 jit_solution(10959959807318060064)
XLA Ops:
  0.6 151.0 %gradients.1 = (bf16[16,3,1536,128]{3,2,1,0:T(8,128)(2,1)S(1)}, f32[8,128]{1,0:T(8,128)}) custom-call(bf16[1,1024,768]{2,1,0:T(8,128)(2,1)} %refs_0_.2, bf16[1,1024,768]{2,1,0:T(8,128)(2,1)} %refs_1_.2, bf16[2,768,2048]{2,1,0:T(8,128)(2,1)} %refs_0_.3, bf16[2,768,2048]{2,1,0:T(8,128)(2,1)} %refs_1_.3, bf16[2,2048,768]{2,1,0:T(8,128)(2,1)} %refs_2_.3), custom_call_target="tpu_custom_call" | custom-call | flops 54760833024 | bytes 37748736 | tf_op jit(solution)/shard_map/gradients/pallas_call | solution.py:506
  151.7 60.9 %adamw.1 = (bf16[2,768,2048]{2,1,0:T(8,128)(2,1)}, bf16[2,768,2048]{2,1,0:T(8,128)(2,1)}, bf16[2,2048,768]{2,1,0:T(8,128)(2,1)}, f32[2,768,2048]{2,1,0:T(8,128)}...) custom-call(f32[8,128]{1,0:T(8,128)} %get-tuple-element.11.squares_r, ...), custom_call_target="tpu_custom_call" | custom-call | tf_op jit(solution)/shard_map/adamw/pallas_call | solution.py:550

commit v2 on v1

--- a/solution.py
+++ b/solution.py
@@ -9,7 +9,7 @@
 
 F32, BF16 = jnp.float32, jnp.bfloat16
 MESH = pl.DeviceIdType.MESH
-SLOTS = 4
+SLOTS = 5
 W = 256
 LANES = 128
 
@@ -66,8 +66,9 @@
 def train_kernel(plan, *refs):
     sizes, tiles, half = plan.sizes, plan.tiles, plan.half
     x_hbm, dy_hbm, gate_hbm, up_hbm, down_hbm = refs[:5]
-    g, squares = refs[5:7]
-    scratch = list(refs[7:])
+    g, squares, down_all, a1_h, turned, p = refs[5:11]
+    scratch = list(refs[11:])
+    a1, h, at_, dt = a1_h.at[0], a1_h.at[1], turned.at[0], turned.at[1]
 
     def take(count):
         out, scratch[:] = scratch[:count], scratch[count:]
@@ -77,8 +78,8 @@
     ring_in, ring_out, pair_in, pair_out, kept, own_in, own_out, own_kept = (take(len(plan.span)) for _ in range(8))
     sq, = take(1)
     recv, send, sq_recv, sq_send_sem = take(4)
-    h, d, a0, a1, at_, dt, acc, p, dg, du, down_all, wg, wu, wd, in_sem, w_sem = take(16)
-    tokens, width = h.shape
+    d, a0, acc, dg, du, wg, wu, wd, in_sem, w_sem, keep_sem = take(11)
+    tokens, width = d.shape
     per = tiles // 2
     rows = min(256, tokens)
 
@@ -225,6 +226,16 @@
         def _():
             tile_forward(after, a0, d)
 
+    def weights_for_adamw(part):
+        if down_all.shape[0] != 2 * tokens:
+            return []
+        if part == 0:
+            pairs = [(down_hbm.at[1, pl.ds(k * tokens, tokens), :], a1_h.at[k]) for k in range(2)]
+        else:
+            pairs = [(gate_hbm.at[1, :, pl.ds(k * tokens, tokens)], turned.at[k]) for k in range(2)]
+            pairs.append((up_hbm.at[1], p.at[pl.ds(0, width), :]))
+        return [pltpu.make_async_copy(src, dst, keep_sem.at[2 * part + k]) for k, (src, dst) in enumerate(pairs)]
+
 
     def sem(array, group, stage, tile):
         return array.at[plan.keys.index((group, stage)), rem(tile, SLOTS)]
@@ -281,7 +292,7 @@
                 put(pair_out[group].at[slot, k - 1, m], pair_in[group].at[rem(tile, R_SLOTS), k - 1, m], group, "p2", tile, device(axes[1], owner))
 
     def exchanged(group, tile):
-        piece, slot, n = plan.piece[group], rem(tile, 4), plan.length[group][2]
+        piece, slot, n = plan.piece[group], rem(tile, SLOTS), plan.length[group][2]
         wait(recv, pair_in[group].at[rem(tile, R_SLOTS)], group, "p2", tile)
         wait(send, pair_out[group].at[rem(tile, 2)], group, "p2", tile)
         for m, (weight, axes) in enumerate(plan.members[group]):
@@ -302,7 +313,7 @@
         return core * half + at[axes[0]] * plan.chunk[group] + at[axes[1]] * plan.piece[group]
 
     def own_step(group, tile):
-        n, slot, last = plan.length[group][2], rem(tile, 4), plan.members[group][0][1][2]
+        n, slot, last = plan.length[group][2], rem(tile, SLOTS), plan.members[group][0][1][2]
 
         @pl.when(at[last] < plan.owners[group])
         def _():
@@ -415,7 +426,7 @@
             sq_send(level + 1)
 
     jobs = [(1, 0, 0, tiles, core_take)]
-    for group in range(len(plan.span)):
+    for group in reversed(range(len(plan.span))):
         def add(delay, part, job, *rest, group=group):
             jobs.append((delay, part, *plan.span[group], lambda tile: job(group, tile, *rest)))
 
@@ -427,6 +438,7 @@
         add(steps + 2, 0, exchanged)
         own = steps + (4 if plan.length[group][2] > 4 else 3)
         add(own, 0, own_step)
+        own += 1 if plan.length[group][2] > 4 else 0
         add(own + 1, 1, spread)
         for step in range(1, steps + 1):
             add(own + 1 + step, 1, gather, step)
@@ -435,7 +447,7 @@
     summed = max(job[0] + job[3] - tiles for job in jobs if job[1] == 0)
     jobs.append((summed, 0, tiles - 1, tiles, lambda tile: sq_send(0)))
     for level in range(4):
-        jobs.append((summed + 1 + level, 1, tiles - 1, tiles, lambda tile, level=level: sq_take(level)))
+        jobs.append((summed + (2, 4, 6, 7)[level], 1, tiles - 1, tiles, lambda tile, level=level: sq_take(level)))
     jobs.sort(key=lambda job: job[0])
     ticks = max(job[0] + job[3] for job in jobs)
 
@@ -463,12 +475,21 @@
             def _():
                 if part:
                     rest(now)
+                    for k, when in enumerate((per, tiles - 1)):
+
+                        @pl.when(now == when)
+                        def _():
+                            for copy in weights_for_adamw(k):
+                                copy.start()
+
                 else:
                     gradients_of(now)
                     core_send(now)
         return carry
 
     lax.fori_loop(0, ticks, tick, 0)
+    for copy in weights_for_adamw(0) + weights_for_adamw(1):
+        copy.wait()
 
 
 S_SLOTS, R_SLOTS = 5, 4
@@ -493,69 +514,90 @@
     scratch += [vmem((R_SLOTS, plan.length[c][1] - 1, count[c], piece[c], LANES), BF16) for c in groups]
     scratch += [vmem((2, plan.length[c][1] - 1, count[c], piece[c], LANES), BF16) for c in groups]
     scratch += [vmem((2, count[c], chunk[c], LANES), F32) for c in groups]
-    scratch += [vmem((4, plan.length[c][2] - 1, count[c], 8, LANES), BF16) for c in groups]
-    scratch += [vmem((4, count[c], piece[c], LANES), BF16) for c in groups]
-    scratch += [vmem((4, count[c], piece[c], LANES), F32) for c in groups]
+    scratch += [vmem((SLOTS, plan.length[c][2] - 1, count[c], 8, LANES), BF16) for c in groups]
+    scratch += [vmem((SLOTS, count[c], piece[c], LANES), BF16) for c in groups]
+    scratch += [vmem((SLOTS, count[c], piece[c], LANES), F32) for c in groups]
     scratch += [vmem((4, 8, 8, LANES), F32)]
     scratch += [dma((len(plan.keys), SLOTS)), dma((len(plan.keys), SLOTS)), dma((4,)), dma((4,))]
-    state, turned = vmem((tokens, width), BF16), vmem((width, tokens), BF16)
-    scratch += [state, state, state, state, turned, turned, vmem((tokens, width), F32)]
-    scratch += [vmem((tokens, hidden), BF16), vmem((tokens, W), BF16), vmem((tokens, W), BF16), vmem((hidden, width), BF16)]
-    scratch += [vmem((4, width, W), BF16), vmem((4, width, W), BF16), vmem((4, W, width), BF16), dma((3,)), dma((4, 3))]
+    scratch += [vmem((tokens, width), BF16), vmem((tokens, width), BF16), vmem((tokens, width), F32), vmem((tokens, W), BF16), vmem((tokens, W), BF16)]
+    scratch += [vmem((4, width, W), BF16), vmem((4, width, W), BF16), vmem((4, W, width), BF16), dma((3,)), dma((4, 3)), dma((5,))]
     flops = 34 * tokens * width * hidden
     return pl.pallas_call(
         functools.partial(train_kernel, plan),
         name="gradients",
-        out_shape=(pltpu.VMEM((tiles, 3, 2 * half, LANES), BF16), jax.ShapeDtypeStruct((8, LANES), F32)),
+        out_shape=(
+            vmem((tiles, 3, 2 * half, LANES), BF16), jax.ShapeDtypeStruct((8, LANES), F32), vmem((hidden, width), BF16),
+            vmem((2, tokens, width), BF16), vmem((2, width, tokens), BF16), vmem((tokens, hidden), BF16),
+        ),
         in_specs=[pl.BlockSpec(memory_space=pl.ANY)] * 5,
-        out_specs=(pl.BlockSpec(memory_space=pltpu.VMEM), pl.BlockSpec(memory_space=pltpu.VMEM)),
+        out_specs=(pl.BlockSpec(memory_space=pltpu.VMEM),) * 6,
         scratch_shapes=scratch,
         cost_estimate=pl.CostEstimate(flops=flops, bytes_accessed=12 * width * hidden * 2, transcendentals=0),
-        compiler_params=pltpu.CompilerParams(collective_id=0, has_side_effects=True, vmem_limit_bytes=48_000_000),
+        compiler_params=pltpu.CompilerParams(collective_id=0, has_side_effects=True, vmem_limit_bytes=34_400_000),
     )(x, dy, *weights)
 
 
-def adamw_kernel(count, squares_ref, g_ref, *refs):
-    ws, ms, vs, new_ws, new_ms, new_vs = (refs[i : i + 3] for i in range(0, 18, 3))
+def adamw_kernel(count, squares_ref, g_ref, down0, down1, gate1, up1, gate0, up0, *refs):
+    ms, vs, new_ws, new_ms, new_vs = (refs[i : i + 3] for i in range(0, 15, 3))
     factor = jnp.minimum(1.0, 0.5 * lax.rsqrt(jnp.sum(squares_ref[...]) / count + 1e-30))
     step = pl.program_id(0)
     per, half, lines = g_ref.shape[0] // 2, g_ref.shape[2] // 2, ms[0].shape[1]
-    first, at = div(step, per) * per, rem(step, per)
-
-    def update(color, g, rows, columns):
-        g = g.astype(F32) * factor
+    at = rem(step, per)
+    mine = pl.ds(pl.multiple_of(at * lines, 8), lines)
+
+    def update(color, g, w, rows, columns):
+        g, w = g.astype(F32) * factor, w.astype(F32)
         m = 0.9 * ms[color][0, rows, columns] + 0.1 * g
         v = 0.95 * vs[color][0, rows, columns] + 0.05 * g * g
-        w = ws[color][0, rows, columns].astype(F32)
         new_ws[color][0, rows, columns] = (w - 0.02 * (m * lax.rsqrt(v + 1e-8) + 0.1 * w)).astype(BF16)
         new_ms[color][0, rows, columns] = m
         new_vs[color][0, rows, columns] = v
 
-    for color in range(2):
-        for t in range(per):
-            for block in range(2):
-                g = g_ref[first + t, color, pl.ds(pl.multiple_of(block * half + at * lines, 8), lines), :]
-                update(color, g, slice(None), pl.ds((2 * t + block) * LANES, LANES))
-    for block in range(2):
-        update(2, g_ref[step, 2, pl.ds(block * half, half), :].astype(F32).T, pl.ds(block * LANES, LANES), slice(None))
-
-
-def adamw(g, squares, weights, m, v):
+    def layer(number):
+        first, split, runs = (1 - number) * per, gate1.shape[2], down1.shape[1] // W
+        for color in range(2):
+            for t in range(per):
+                for block in range(2):
+                    g = g_ref[first + t, color, pl.ds(pl.multiple_of(block * half + at * lines, 8), lines), :]
+                    column = (2 * t + block) * LANES
+                    columns = pl.ds(column, LANES)
+                    if number == 0:
+                        w = (gate0, up0)[color][0, :, columns]
+                    elif color == 0:
+                        w = gate1[column // split, mine, pl.ds(column % split, LANES)]
+                    else:
+                        w = up1[mine, columns]
+                    update(color, g, w, slice(None), columns)
+        for block in range(2):
+            g = g_ref[first + at, 2, pl.ds(block * half, half), :].astype(F32).T
+            if number == 0:
+                w = down0[pl.ds(pl.multiple_of(at * W + block * LANES, 8), LANES), :]
+            else:
+                w = down1[div(at, runs), pl.ds(pl.multiple_of(rem(at, runs) * W + block * LANES, 8), LANES), :]
+            update(2, g, w, pl.ds(block * LANES, LANES), slice(None))
+
+    pl.when(step < per)(functools.partial(layer, 1))
+    pl.when(step >= per)(functools.partial(layer, 0))
+
+
+def adamw(g, squares, kept, weights, m, v):
     tiles, half = g.shape[0], g.shape[2] // 2
     per = tiles // 2
     up = pl.BlockSpec((1, half // per, W * per), lambda i: (1 - i // per, i % per, 0))
     down = pl.BlockSpec((1, W, half), lambda i: (1 - i // per, i % per, 0))
-    three = [up, up, down]
+    later = pl.BlockSpec((1, half // per, W * per), lambda i: (0, jnp.maximum(i - per, 0), 0))
+    here = pl.BlockSpec(memory_space=pltpu.VMEM)
     out = [jax.ShapeDtypeStruct(a.shape, a.dtype) for a in (*weights, *m, *v)]
+    in_vmem = [pltpu.with_memory_space_constraint(a, pltpu.VMEM) for a in (g, *kept)]
     return pl.pallas_call(
         functools.partial(adamw_kernel, float(sum(w.size for w in weights))),
         name="adamw",
         grid=(tiles,),
         out_shape=out,
-        in_specs=[pl.BlockSpec(squares.shape, lambda i: (0, 0)), pl.BlockSpec(memory_space=pltpu.VMEM)] + three * 3,
-        out_specs=three * 3,
-        compiler_params=pltpu.CompilerParams(vmem_limit_bytes=48_000_000),
-    )(squares, pltpu.with_memory_space_constraint(g, pltpu.VMEM), *weights, *m, *v)
+        in_specs=[pl.BlockSpec(squares.shape, lambda i: (0, 0))] + [here] * 5 + [later] * 2 + [up, up, down] * 2,
+        out_specs=[up, up, down] * 3,
+        compiler_params=pltpu.CompilerParams(vmem_limit_bytes=34_400_000),
+    )(squares, *in_vmem, *weights[:2], *m, *v)
 
 
 def solution(mesh):
@@ -563,8 +605,8 @@
 
     def step(x, dy, *arrays):
         weights, m, v = (arrays[i : i + 3] for i in (0, 3, 6))
-        g, squares = gradients(plan, x, dy, weights)
-        return tuple(adamw(g, squares, weights, m, v))
+        g, squares, *kept = gradients(plan, x, dy, weights)
+        return tuple(adamw(g, squares, kept, weights, m, v))
 
     return jax.shard_map(
         step,

time: 213 us -> 217 us (1.019)
  Pallas kernels: 212 us -> 216 us
    pallas_call x1, Pallas kernels: 60.9 us -> 69.4 us  [adamw(): pl.pallas_call(functools.partial(adamw_kernel, float(sum((w.size for w in...]
    pallas_call x1, Pallas kernels: 151 us -> 147 us  [gradients(): pl.pallas_call(functools.partial(train_kernel, plan), name='gradients', o...]
where the time goes in v2:
time: 217 us
  Pallas kernels  216 us (100%)
    pallas_call x1, Pallas kernels, gradients(): pl.pallas_call(functools.partial(train_kernel, plan), name='gradients', o...  147 us
    pallas_call x1, Pallas kernels, adamw(): pl.pallas_call(functools.partial(adamw_kernel, float(sum((w.size for w in...  69.4 us

profile of v2, /device:TPU:1, one launch (start us, length us, event | category | flops | bytes accessed | tf_op | source)
XLA Modules:
  0.0 217.2 jit_solution(13926299490372824995)
XLA Ops:
  0.6 146.9 %gradients.1 = (bf16[16,3,1536,128]{3,2,1,0:T(8,128)(2,1)S(1)}, f32[8,128]{1,0:T(8,128)}, bf16[2048,768]{1,0:T(8,128)(2,1)S(1)}, bf16[2,1024,768]{2,1,0:T(8,128)...) custom-call(bf16[1,1024,768]{2,1,0:T(8,128)(2,1)} %refs_0_.2, ...), custom_call_target="tpu_custom_call" | custom-call | flops 54760833024 | bytes 37748736 | tf_op jit(solution)/shard_map/gradients/pallas_call | solution.py:525
  147.6 69.4 %adamw.1 = (bf16[2,768,2048]{2,1,0:T(8,128)(2,1)}, bf16[2,768,2048]{2,1,0:T(8,128)(2,1)}, bf16[2,2048,768]{2,1,0:T(8,128)(2,1)}, f32[2,768,2048]{2,1,0:T(8,128)}...) custom-call(f32[8,128]{1,0:T(8,128)} %get-tuple-element.15.squares_r, ...), custom_call_target="tpu_custom_call" | custom-call | tf_op jit(solution)/shard_map/adamw/pallas_call | solution.py:592

commit v3 on v1

--- a/solution.py
+++ b/solution.py
@@ -9,7 +9,7 @@
 
 F32, BF16 = jnp.float32, jnp.bfloat16
 MESH = pl.DeviceIdType.MESH
-SLOTS = 4
+SLOTS = 5
 W = 256
 LANES = 128
 
@@ -281,7 +281,7 @@
                 put(pair_out[group].at[slot, k - 1, m], pair_in[group].at[rem(tile, R_SLOTS), k - 1, m], group, "p2", tile, device(axes[1], owner))
 
     def exchanged(group, tile):
-        piece, slot, n = plan.piece[group], rem(tile, 4), plan.length[group][2]
+        piece, slot, n = plan.piece[group], rem(tile, SLOTS), plan.length[group][2]
         wait(recv, pair_in[group].at[rem(tile, R_SLOTS)], group, "p2", tile)
         wait(send, pair_out[group].at[rem(tile, 2)], group, "p2", tile)
         for m, (weight, axes) in enumerate(plan.members[group]):
@@ -302,7 +302,7 @@
         return core * half + at[axes[0]] * plan.chunk[group] + at[axes[1]] * plan.piece[group]
 
     def own_step(group, tile):
-        n, slot, last = plan.length[group][2], rem(tile, 4), plan.members[group][0][1][2]
+        n, slot, last = plan.length[group][2], rem(tile, SLOTS), plan.members[group][0][1][2]
 
         @pl.when(at[last] < plan.owners[group])
         def _():
@@ -415,7 +415,7 @@
             sq_send(level + 1)
 
     jobs = [(1, 0, 0, tiles, core_take)]
-    for group in range(len(plan.span)):
+    for group in reversed(range(len(plan.span))):
         def add(delay, part, job, *rest, group=group):
             jobs.append((delay, part, *plan.span[group], lambda tile: job(group, tile, *rest)))
 
@@ -427,6 +427,7 @@
         add(steps + 2, 0, exchanged)
         own = steps + (4 if plan.length[group][2] > 4 else 3)
         add(own, 0, own_step)
+        own += 1 if plan.length[group][2] > 4 else 0
         add(own + 1, 1, spread)
         for step in range(1, steps + 1):
             add(own + 1 + step, 1, gather, step)
@@ -435,7 +436,7 @@
     summed = max(job[0] + job[3] - tiles for job in jobs if job[1] == 0)
     jobs.append((summed, 0, tiles - 1, tiles, lambda tile: sq_send(0)))
     for level in range(4):
-        jobs.append((summed + 1 + level, 1, tiles - 1, tiles, lambda tile, level=level: sq_take(level)))
+        jobs.append((summed + (2, 4, 6, 7)[level], 1, tiles - 1, tiles, lambda tile, level=level: sq_take(level)))
     jobs.sort(key=lambda job: job[0])
     ticks = max(job[0] + job[3] for job in jobs)
 
@@ -493,9 +494,9 @@
     scratch += [vmem((R_SLOTS, plan.length[c][1] - 1, count[c], piece[c], LANES), BF16) for c in groups]
     scratch += [vmem((2, plan.length[c][1] - 1, count[c], piece[c], LANES), BF16) for c in groups]
     scratch += [vmem((2, count[c], chunk[c], LANES), F32) for c in groups]
-    scratch += [vmem((4, plan.length[c][2] - 1, count[c], 8, LANES), BF16) for c in groups]
-    scratch += [vmem((4, count[c], piece[c], LANES), BF16) for c in groups]
-    scratch += [vmem((4, count[c], piece[c], LANES), F32) for c in groups]
+    scratch += [vmem((SLOTS, plan.length[c][2] - 1, count[c], 8, LANES), BF16) for c in groups]
+    scratch += [vmem((SLOTS, count[c], piece[c], LANES), BF16) for c in groups]
+    scratch += [vmem((SLOTS, count[c], piece[c], LANES), F32) for c in groups]
     scratch += [vmem((4, 8, 8, LANES), F32)]
     scratch += [dma((len(plan.keys), SLOTS)), dma((len(plan.keys), SLOTS)), dma((4,)), dma((4,))]
     state, turned = vmem((tokens, width), BF16), vmem((width, tokens), BF16)

time: 213 us -> 209 us (0.981)
  Pallas kernels: 212 us -> 208 us
    pallas_call x1, Pallas kernels: 151 us -> 147 us  [gradients(): pl.pallas_call(functools.partial(train_kernel, plan), name='gradients', o...]
where the time goes in v3:
time: 209 us; the launch traced here: 208 us
  Pallas kernels  208 us (100%)
    pallas_call x1, Pallas kernels, gradients(): pl.pallas_call(functools.partial(train_kernel, plan), name='gradients', o...  147 us
    pallas_call x1, Pallas kernels, adamw(): pl.pallas_call(functools.partial(adamw_kernel, float(sum((w.size for w in...  60.9 us

profile of v3, /device:TPU:1, one launch (start us, length us, event | category | flops | bytes accessed | tf_op | source)
XLA Modules:
  0.0 208.5 jit_solution(16455184200465533471)
XLA Ops:
  0.6 146.7 %gradients.1 = (bf16[16,3,1536,128]{3,2,1,0:T(8,128)(2,1)S(1)}, f32[8,128]{1,0:T(8,128)}) custom-call(bf16[1,1024,768]{2,1,0:T(8,128)(2,1)} %refs_0_.2, bf16[1,1024,768]{2,1,0:T(8,128)(2,1)} %refs_1_.2, bf16[2,768,2048]{2,1,0:T(8,128)(2,1)} %refs_0_.3, bf16[2,768,2048]{2,1,0:T(8,128)(2,1)} %refs_1_.3, bf16[2,2048,768]{2,1,0:T(8,128)(2,1)} %refs_2_.3), custom_call_target="tpu_custom_call" | custom-call | flops 54760833024 | bytes 37748736 | tf_op jit(solution)/shard_map/gradients/pallas_call | solution.py:507
  147.4 60.9 %adamw.1 = (bf16[2,768,2048]{2,1,0:T(8,128)(2,1)}, bf16[2,768,2048]{2,1,0:T(8,128)(2,1)}, bf16[2,2048,768]{2,1,0:T(8,128)(2,1)}, f32[2,768,2048]{2,1,0:T(8,128)}...) custom-call(f32[8,128]{1,0:T(8,128)} %get-tuple-element.11.squares_r, ...), custom_call_target="tpu_custom_call" | custom-call | tf_op jit(solution)/shard_map/adamw/pallas_call | solution.py:551

commit v4 on v3

--- a/solution.py
+++ b/solution.py
@@ -146,17 +146,20 @@
             d[block, :] = (d[block, :].astype(F32) + by_h.astype(BF16).astype(F32)).astype(BF16)
 
     def forward():
-        load_x = pltpu.make_async_copy(x_hbm.at[0], h, in_sem.at[0])
+        load_x = [
+            pltpu.make_async_copy(x_hbm.at[0, pl.ds(r, rows), :], h.at[pl.ds(r, rows), :], in_sem.at[3 + r // rows]) for r in range(0, tokens, rows)
+        ]
         load_dy = pltpu.make_async_copy(dy_hbm.at[0], d, in_sem.at[1])
         load_down = pltpu.make_async_copy(down_hbm.at[0], down_all, in_sem.at[2])
-        load_x.start()
+        for copy in load_x:
+            copy.start()
         for t in range(2):
             fetch(0, t, t, True, False)
+        for r in range(0, tokens, rows):
+            load_x[r // rows].wait()
+            a0[r : r + rows, :] = normed(h[r : r + rows, :])
         load_down.start()
         load_dy.start()
-        load_x.wait()
-        for r in range(0, tokens, rows):
-            a0[r : r + rows, :] = normed(h[r : r + rows, :])
 
         def pair(i, carry):
             base = 2 * rem(i, 2)
@@ -502,7 +505,7 @@
     state, turned = vmem((tokens, width), BF16), vmem((width, tokens), BF16)
     scratch += [state, state, state, state, turned, turned, vmem((tokens, width), F32)]
     scratch += [vmem((tokens, hidden), BF16), vmem((tokens, W), BF16), vmem((tokens, W), BF16), vmem((hidden, width), BF16)]
-    scratch += [vmem((4, width, W), BF16), vmem((4, width, W), BF16), vmem((4, W, width), BF16), dma((3,)), dma((4, 3))]
+    scratch += [vmem((4, width, W), BF16), vmem((4, width, W), BF16), vmem((4, W, width), BF16), dma((3 + tokens // min(256, tokens),)), dma((4, 3))]
     flops = 34 * tokens * width * hidden
     return pl.pallas_call(
         functools.partial(train_kernel, plan),

time: 209 us -> 209 us (level)
  no operation moved by 1% of the time
where the time goes in v4:
time: 209 us
  Pallas kernels  208 us (100%)
    pallas_call x1, Pallas kernels, gradients(): pl.pallas_call(functools.partial(train_kernel, plan), name='gradients', o...  147 us
    pallas_call x1, Pallas kernels, adamw(): pl.pallas_call(functools.partial(adamw_kernel, float(sum((w.size for w in...  60.9 us

profile of v4, /device:TPU:1, one launch (start us, length us, event | category | flops | bytes accessed | tf_op | source)
XLA Modules:
  0.0 208.5 jit_solution(7196523984827273609)
XLA Ops:
  0.6 146.8 %gradients.1 = (bf16[16,3,1536,128]{3,2,1,0:T(8,128)(2,1)S(1)}, f32[8,128]{1,0:T(8,128)}) custom-call(bf16[1,1024,768]{2,1,0:T(8,128)(2,1)} %refs_0_.2, bf16[1,1024,768]{2,1,0:T(8,128)(2,1)} %refs_1_.2, bf16[2,768,2048]{2,1,0:T(8,128)(2,1)} %refs_0_.3, bf16[2,768,2048]{2,1,0:T(8,128)(2,1)} %refs_1_.3, bf16[2,2048,768]{2,1,0:T(8,128)(2,1)} %refs_2_.3), custom_call_target="tpu_custom_call" | custom-call | flops 54760833024 | bytes 37748736 | tf_op jit(solution)/shard_map/gradients/pallas_call | solution.py:510
  147.4 60.9 %adamw.1 = (bf16[2,768,2048]{2,1,0:T(8,128)(2,1)}, bf16[2,768,2048]{2,1,0:T(8,128)(2,1)}, bf16[2,2048,768]{2,1,0:T(8,128)(2,1)}, f32[2,768,2048]{2,1,0:T(8,128)}...) custom-call(f32[8,128]{1,0:T(8,128)} %get-tuple-element.11.squares_r, ...), custom_call_target="tpu_custom_call" | custom-call | tf_op jit(solution)/shard_map/adamw/pallas_call | solution.py:554
